TPU v7x, 128 devices: a whole 4x4x4 slice. The times are simulated.
128 devices in a mesh: rep: 1, r: 4 (over x), s: 32 (over y, z, core).
Axes of the slice: x: 4, y: 4, z: 4, core: 2. Of those that a mesh axis runs over, the one named last changes fastest.
Arguments:
- x: bfloat16 [128, 2048, 1280], P(('rep', 'r', 's'))
- dy: bfloat16 [128, 2048, 1280], P(('rep', 'r', 's'))
- w_gate: bfloat16 [2, 1280, 4480], P(None, 's')
- w_up: bfloat16 [2, 1280, 4480], P(None, 's')
- w_down: bfloat16 [2, 4480, 1280], P(None, 's')
- m_w_gate: float32 [2, 1280, 4480], P(None, 's')
- m_w_up: float32 [2, 1280, 4480], P(None, 's')
- m_w_down: float32 [2, 4480, 1280], P(None, 's')
- v_w_gate: float32 [2, 1280, 4480], P(None, 's')
- v_w_up: float32 [2, 1280, 4480], P(None, 's')
- v_w_down: float32 [2, 4480, 1280], P(None, 's')
Outputs:
- output 1: bfloat16 [2, 1280, 4480], P('rep', 's')
- output 2: bfloat16 [2, 1280, 4480], P('rep', 's')
- output 3: bfloat16 [2, 4480, 1280], P('rep', 's')
- output 4: float32 [2, 1280, 4480], P('rep', 's')
- output 5: float32 [2, 1280, 4480], P('rep', 's')
- output 6: float32 [2, 4480, 1280], P('rep', 's')
- output 7: float32 [2, 1280, 4480], P('rep', 's')
- output 8: float32 [2, 1280, 4480], P('rep', 's')
- output 9: float32 [2, 4480, 1280], P('rep', 's')
All inputs are finite; a program needn't handle non-finite values.
Results may differ from a plain program's by a relative error of at most 0.022.
Values are sent between devices in bfloat16 or wider.
A program may use at most 1.5 GiB of HBM per device.

v0:
```python
import jax
import jax.numpy as jnp
from jax import lax
from jax.sharding import PartitionSpec as P

NAMES = ("w_gate", "w_up", "w_down")


def matmul(a, w):
    return jnp.dot(a, w, preferred_element_type=jnp.float32).astype(jnp.bfloat16)


def normed(h):
    wide = h.astype(jnp.float32)
    scale = lax.rsqrt(jnp.mean(wide**2, -1, keepdims=True) + 1e-6)
    return (wide * scale).astype(jnp.bfloat16)


def layer(h, w):
    a = normed(h)
    gate = jnp.dot(a, w["w_gate"], preferred_element_type=jnp.float32)
    up = jnp.dot(a, w["w_up"], preferred_element_type=jnp.float32)
    return h + matmul((jax.nn.silu(gate) * up).astype(jnp.bfloat16), w["w_down"])


def adamw(w, m, v, g):
    m = 0.9 * m + 0.1 * g
    v = 0.95 * v + 0.05 * g * g
    step = m * lax.rsqrt(v + 1e-8) + 0.1 * w
    return (w - 0.02 * step).astype(jnp.bfloat16), m, v


def solution(mesh):
    def fetched(weights, number):
        return {name: lax.all_gather(w[number], "s", axis=0, tiled=True) for name, w in zip(NAMES, weights, strict=True)}

    def summed(term):
        return lax.psum(lax.psum_scatter(term, "s", scatter_dimension=0, tiled=True), "r")

    def step(x, dy, *arrays):
        weights, m, v = (arrays[i : i + 3] for i in (0, 3, 6))
        layers = weights[0].shape[0]
        h, kept = x[0], []
        for number in range(layers):
            kept.append(h)
            h = layer(h, fetched(weights, number))
        by_h, mine = dy[0], [None] * layers
        for number in reversed(range(layers)):
            _, back = jax.vjp(lambda w, h: layer(h, w), fetched(weights, number), kept[number])
            by_w, by_h = back(by_h)
            mine[number] = [summed(by_w[name]) for name in NAMES]
        gradients = [jnp.stack([mine[number][i] for number in range(layers)]).astype(jnp.float32) for i in range(3)]
        new = [adamw(w.astype(jnp.float32), m, v, g) for w, m, v, g in zip(weights, m, v, gradients, strict=True)]
        return tuple(one[which] for which in range(3) for one in new)

    states, cut = P(("rep", "r", "s"), None, None), P(None, "s", None)
    return jax.shard_map(
        step,
        mesh=mesh,
        in_specs=(states, states) + (cut,) * 9,
        out_specs=(P("rep", "s", None),) * 9,
        check_vma=False,
    )
```

profile of v0, /device:TPU:1, one launch (start us, length us, event | category | flops | bytes accessed | tf_op | source)
XLA Modules:
  0.0 1324.1 jit_solution(2442107072996643057)
XLA Ops:
  7.2 0.0 all-gather.13.cloned.1.call-start
  7.2 2.0 fusion.103
  9.2 0.0 all-gather.15.cloned.1.call-start
  9.3 2.0 fusion.102
  11.3 0.0 all-gather.17.cloned.1.call-start
  11.4 3.7 fusion.101
  15.0 0.0 all-gather.17.cloned.1.call-update
  15.1 0.0 all-gather.21.cloned.1.call-start
  15.1 0.5 all-gather.21.cloned.1.call-update
  15.6 0.0 all-gather.23.cloned.1.call-start
  15.7 0.5 all-gather.23.cloned.1.call-update
  16.2 0.0 all-gather.19.cloned.1.call-start
  16.3 0.5 all-gather.19.cloned.1.call-update
  16.8 0.0 reduce-scatter.21.cloned.1.call-start
  16.9 7.9 copy.38
  24.8 3.6 fusion.37
  28.4 8.0 copy.39
  36.4 37.9 %all-gather.13.cloned.1.call-done = bf16[1,1280,4480]{2,1,0:T(8,128)(2,1)} async-done(((bf16[1,40,4480]{2,1,0:T(8,128)(2,1)}), bf16[1,1280,4480]{2,1,0:T(8,128)(2,1)}) %all-gather.13.cloned.1.call-update) | async-done | bytes 11468816 | tf_op jit(solution)/shard_map/all_gather | solution.py:35
  74.3 32.1 %fusion.35 = f32[2048,4480]{1,0:T(8,128)} fusion(bf16[1,1280,4480]{2,1,0:T(8,128)(2,1)} %all-gather.13.cloned.1.call-done, bf16[1,2048,1280]{1,2,0:T(8,128)(2,1)} %copy.38, f32[2048]{0:T(1024)S(1)} %add_rsqrt_fusion), kind=kOutput, calls=%fused_computation.52 | convolution fusion | flops 23495966720 | bytes 53420032 | tf_op jit(solution)/shard_map/dot_general | solution.py:21
  106.4 30.1 %all-gather.15.cloned.1.call-done = bf16[1,1280,4480]{2,1,0:T(8,128)(2,1)} async-done(((bf16[1,40,4480]{2,1,0:T(8,128)(2,1)}), bf16[1,1280,4480]{2,1,0:T(8,128)(2,1)}) %all-gather.15.cloned.1.call-update) | async-done | bytes 11468816 | tf_op jit(solution)/shard_map/all_gather | solution.py:35
  136.4 45.2 %multiply_convert_fusion.1 = (bf16[2048,4480]{1,0:T(8,128)(2,1)}, f32[2048,4480]{1,0:T(8,128)}) fusion(f32[2048,4480]{1,0:T(8,128)} %fusion.35, bf16[1,1280,4480]{2,1,0:T(8,128)(2,1)} %all-gather.15.cloned.1.call-done, bf16[1,2048,1280]{1,2,0:T(8,128)(2,1)} %copy.38, f32[2048]{0:T(1024)S(1)} %add_rsqrt_fusion), kind=kOutput, calls=%fused_computation.17 | convolution fusion | flops 23551016960 | bytes 108470272 | tf_op jit(solution)/shard_map/dot_general | solution.py:22
  181.7 43.8 %all-gather.17.cloned.1.call-done = bf16[1,4480,1280]{2,0,1:T(2,128)(2,1)} async-done(((bf16[1,140,1280]{2,0,1:T(2,128)(2,1)}), bf16[1,4480,1280]{2,0,1:T(2,128)(2,1)}) %all-gather.17.cloned.1.call-update) | async-done | bytes 11468816 | tf_op jit(solution)/shard_map/all_gather | solution.py:35
  225.5 46.5 %fusion.41 = (f32[2048]{0:T(1024)S(1)}, bf16[2048,1280]{0,1:T(8,128)(2,1)}) fusion(bf16[2048,4480]{1,0:T(8,128)(2,1)} %get-tuple-element.61, bf16[1,4480,1280]{2,0,1:T(2,128)(2,1)} %all-gather.17.cloned.1.call-done, bf16[1,2048,1280]{1,2,0:T(8,128)(2,1)} %copy.38), kind=kOutput, calls=%fused_computation.58 | convolution fusion | flops 23501207552 | bytes 40312832 | tf_op jit(solution)/shard_map/dot_general | solution.py:10
  271.9 42.3 %all-gather.21.cloned.1.call-done = bf16[1,4480,1280]{2,0,1:T(2,128)(2,1)} async-done(((bf16[1,140,1280]{2,0,1:T(2,128)(2,1)}), bf16[1,4480,1280]{2,0,1:T(2,128)(2,1)}) %all-gather.21.cloned.1.call-update) | async-done | bytes 11468816 | tf_op jit(solution)/shard_map/all_gather | solution.py:35
  314.2 33.1 %convolution_convert_fusion.1 = bf16[2048,4480]{1,0:T(8,128)(2,1)} fusion(bf16[1,4480,1280]{2,0,1:T(2,128)(2,1)} %all-gather.21.cloned.1.call-done, bf16[1,2048,1280]{2,1,0:T(8,128)(2,1)} %param.12), kind=kOutput, calls=%fused_computation.26 | convolution fusion | flops 23497277440 | bytes 35061760 | tf_op jit(solution)/shard_map/transpose(jvp())/dot_general | solution.py:10
  347.3 28.8 %all-gather.23.cloned.1.call-done = bf16[1,1280,4480]{2,1,0:T(8,128)(2,1)} async-done(((bf16[1,40,4480]{2,1,0:T(8,128)(2,1)}), bf16[1,1280,4480]{2,1,0:T(8,128)(2,1)}) %all-gather.23.cloned.1.call-update) | async-done | bytes 11468816 | tf_op jit(solution)/shard_map/all_gather | solution.py:35
  376.1 32.0 %fusion.26 = f32[2048,4480]{1,0:T(8,128)} fusion(bf16[1,1280,4480]{2,1,0:T(8,128)(2,1)} %all-gather.23.cloned.1.call-done, bf16[2048,1280]{0,1:T(8,128)(2,1)} %get-tuple-element.64, f32[2048]{0:T(1024)S(1)} %fusion.88), kind=kOutput, calls=%fused_computation.43 | convolution fusion | flops 23495966720 | bytes 53420032 | tf_op jit(solution)/shard_map/jvp()/dot_general | solution.py:22
  408.1 30.0 %all-gather.19.cloned.1.call-done = bf16[1,1280,4480]{2,1,0:T(8,128)(2,1)} async-done(((bf16[1,40,4480]{2,1,0:T(8,128)(2,1)}), bf16[1,1280,4480]{2,1,0:T(8,128)(2,1)}) %all-gather.19.cloned.1.call-update) | async-done | bytes 11468816 | tf_op jit(solution)/shard_map/all_gather | solution.py:35
  438.1 54.5 %fusion.4 = (bf16[2048,4480]{1,0:T(8,128)(2,1)}, f32[2048,4480]{1,0:T(8,128)}) fusion(f32[2048,4480]{1,0:T(8,128)} %fusion.26, bf16[2048,4480]{1,0:T(8,128)(2,1)} %convolution_convert_fusion.1, bf16[1,1280,4480]{2,1,0:T(8,128)(2,1)} %all-gather.19.cloned.1.call-done, bf16[2048,1280]{0,1:T(8,128)(2,1)} %get-tuple-element.64, f32[2048]{0:T(1024)S(1)} %fusion.88), kind=kOutput, calls=%fused_computation.8 | convolution fusion | flops 23606067200 | bytes 126820352 | tf_op jit(solution)/shard_map/jvp()/dot_general | solution.py:21
  492.6 35.5 %fusion.47 = bf16[2048,1280]{0,1:T(8,128)(2,1)} fusion(bf16[1,1280,4480]{2,1,0:T(8,128)(2,1)} %all-gather.23.cloned.1.call-done, bf16[2048,4480]{1,0:T(8,128)(2,1)} %convolution_convert_fusion.1, f32[2048,4480]{1,0:T(8,128)} %get-tuple-element.66), kind=kOutput, calls=%fused_computation.62 | convolution fusion | flops 23545774080 | bytes 71761920 | tf_op jit(solution)/shard_map/transpose(jvp())/dot_general | solution.py:22
  528.0 34.2 %fusion.43 = (f32[2048]{0:T(1024)S(1)}, bf16[2048,1280]{0,1:T(8,128)(2,1)}) fusion(bf16[2048,1280]{0,1:T(8,128)(2,1)} %get-tuple-element.64, bf16[2048,1280]{0,1:T(8,128)(2,1)} %fusion.47, bf16[2048,4480]{1,0:T(8,128)(2,1)} %get-tuple-element.65, bf16[1,1280,4480]{2,1,0:T(8,128)(2,1)} %all-gather.19.cloned.1.call-done), kind=kOutput, calls=%fused_computation.60 | convolution fusion | flops 23501207552 | bytes 45555712 | tf_op jit(solution)/shard_map/transpose(jvp())/dot_general | solution.py:21
  562.3 12.3 fusion.60
  574.6 33.0 %convolution_convert_fusion = bf16[2048,4480]{1,0:T(8,128)(2,1)} fusion(bf16[2048,1280]{0,1:T(8,128)(2,1)} %fusion.60, bf16[1,4480,1280]{2,0,1:T(2,128)(2,1)} %all-gather.17.cloned.1.call-done), kind=kOutput, calls=%fused_computation.25 | convolution fusion | flops 23497277440 | bytes 35061760 | tf_op jit(solution)/shard_map/transpose(jvp())/dot_general | solution.py:10
  607.6 37.4 %fusion.19 = bf16[1280,4480]{1,0:T(8,128)(2,1)} fusion(bf16[2048,4480]{1,0:T(8,128)(2,1)} %convolution_convert_fusion, f32[2048,4480]{1,0:T(8,128)} %fusion.35, bf16[1,2048,1280]{1,2,0:T(8,128)(2,1)} %copy.38, f32[2048]{0:T(1024)S(1)} %copy-done.14), kind=kOutput, calls=%fused_computation.24 | convolution fusion | flops 23556751360 | bytes 71770112 | tf_op jit(solution)/shard_map/transpose(jvp())/dot_general | solution.py:22
  645.0 0.0 reduce-scatter.23.cloned.1.call-start
  645.1 37.7 %fusion.15 = bf16[1280,4480]{1,0:T(8,128)(2,1)} fusion(bf16[2048,4480]{1,0:T(8,128)(2,1)} %convolution_convert_fusion.1, bf16[2048,1280]{0,1:T(8,128)(2,1)} %get-tuple-element.64, f32[2048]{0:T(1024)S(1)} %fusion.88, f32[2048,4480]{1,0:T(8,128)} %get-tuple-element.66), kind=kOutput, calls=%fused_computation.22 | convolution fusion | flops 23556751360 | bytes 71770112 | tf_op jit(solution)/shard_map/transpose(jvp())/dot_general | solution.py:22
  682.8 0.0 reduce-scatter.17.cloned.1.call-start
  682.8 44.7 %fusion.16 = bf16[1280,4480]{1,0:T(8,128)(2,1)} fusion(f32[2048,4480]{1,0:T(8,128)} %fusion.35, f32[2048,4480]{1,0:T(8,128)} %get-tuple-element.62, bf16[2048,4480]{1,0:T(8,128)(2,1)} %convolution_convert_fusion, bf16[1,2048,1280]{1,2,0:T(8,128)(2,1)} %copy.38, f32[2048]{0:T(1024)S(1)} %copy-done.14), kind=kOutput, calls=%fused_computation.23 | convolution fusion | flops 23602626560 | bytes 108470272 | tf_op jit(solution)/shard_map/transpose(jvp())/dot_general | solution.py:21
  727.5 0.0 reduce-scatter.19.cloned.1.call-start
  727.5 31.2 %convolution_convert_fusion.4 = bf16[1280,4480]{1,0:T(8,128)(2,1)} fusion(bf16[2048,4480]{1,0:T(8,128)(2,1)} %get-tuple-element.65, bf16[2048,1280]{0,1:T(8,128)(2,1)} %get-tuple-element.64, f32[2048]{0:T(1024)S(1)} %fusion.88), kind=kOutput, calls=%fused_computation.29 | convolution fusion | flops 23495966720 | bytes 35069952 | tf_op jit(solution)/shard_map/transpose(jvp())/dot_general | solution.py:21
  758.8 0.0 all-reduce.12.cloned.1.call-start
  758.8 30.1 %convolution_convert_fusion.3 = bf16[4480,1280]{1,0:T(8,128)(2,1)} fusion(bf16[2048,4480]{1,0:T(8,128)(2,1)} %get-tuple-element.61, bf16[2048,1280]{0,1:T(8,128)(2,1)} %fusion.60), kind=kOutput, calls=%fused_computation.28 | convolution fusion | flops 23493836800 | bytes 35061760 | tf_op jit(solution)/shard_map/transpose(jvp())/dot_general | solution.py:10
  788.9 38.4 %convolution_convert_fusion.2 = bf16[4480,1280]{1,0:T(8,128)(2,1)} fusion(f32[2048,4480]{1,0:T(8,128)} %fusion.26, bf16[1,2048,1280]{2,1,0:T(8,128)(2,1)} %param.12, f32[2048,4480]{1,0:T(8,128)} %get-tuple-element.66), kind=kOutput, calls=%fused_computation.27 | convolution fusion | flops 23548887040 | bytes 90112000 | tf_op jit(solution)/shard_map/transpose(jvp())/dot_general | solution.py:10
  827.3 146.1 %fusion.94 = (bf16[144,1280]{1,0:T(8,128)(2,1)S(1)}, bf16[144,1280]{1,0:T(8,128)(2,1)S(1)}) fusion(bf16[4480,1280]{1,0:T(8,128)(2,1)} %convolution_convert_fusion.2, bf16[4480,1280]{1,0:T(8,128)(2,1)} %convolution_convert_fusion.3), kind=kCustom, calls=%all-reduce-scatter.2 | all-reduce-scatter fusion | flops 11796481 | bytes 23675392
  973.4 0.1 slice.27
  973.5 4.4 collective-permute-start
  977.9 0.1 slice.28
  978.0 1.9 collective-permute-start.1
  979.9 0.6 dynamic-slice.14
  981.2 0.7 collective-permute-done
  981.9 1.5 concatenate
  983.4 2.0 collective-permute-done.1
  985.4 5.3 concatenate.1
  990.7 0.8 dynamic-slice_bitcast_fusion.1
  991.5 1.8 dynamic-slice_bitcast_fusion
  993.4 8.4 reduce-scatter.23.cloned.1.call-done
  1001.8 119.4 %reduce-scatter.17.cloned.1.call-done = bf16[40,4480]{1,0:T(8,128)(2,1)} async-done(((bf16[1280,4480]{1,0:T(8,128)(2,1)}), bf16[40,4480]{1,0:T(8,128)(2,1)}) %reduce-scatter.17.cloned.1.call-update) | async-done | bytes 358416
  1121.2 119.2 %reduce-scatter.19.cloned.1.call-done = bf16[40,4480]{1,0:T(8,128)(2,1)} async-done(((bf16[1280,4480]{1,0:T(8,128)(2,1)}), bf16[40,4480]{1,0:T(8,128)(2,1)}) %reduce-scatter.19.cloned.1.call-update) | async-done | bytes 358416
  1240.5 63.9 %all-reduce.12.cloned.1.call-done = (bf16[1,40,4480]{2,1,0:T(8,128)(2,1)}, bf16[1,40,4480]{2,1,0:T(8,128)(2,1)}, bf16[1,40,4480]{2,1,0:T(8,128)(2,1)}, bf16[1,40...) async-done(((bf16[1,40,4480]{2,1,0:T(8,128)(2,1)}, bf16[1,40,4480]{2,1,0:T(8,128)(2,1)}, bf16[1,40,4480]{2,1,0:T(8,128)(2,1)}, ...) | async-done | bytes 2150416 | tf_op jit(solution)/shard_map/psum | solution.py:38
  1304.5 3.0 fusion.75
  1307.4 2.2 copy.44
  1309.6 2.2 copy.45
  1311.9 1.4 copy.43
  1313.3 3.8 fusion.80
  (43 shorter events, 0.2 us)
Async XLA Ops:
  7.2 67.1 %all-gather.13.cloned.1.call-start = ((), (), s32[]{:S(2)}) async-start(), calls=%async_computation.4 | async-start | bytes 11827200 | tf_op jit(solution)/shard_map/all_gather | solution.py:35
  9.2 127.2 %all-gather.15.cloned.1.call-start = ((), (), s32[]{:S(2)}) async-start(), calls=%async_computation.5 | async-start | bytes 11827200 | tf_op jit(solution)/shard_map/all_gather | solution.py:35
  11.3 214.1 %all-gather.17.cloned.1.call-start = ((), (), s32[]{:S(2)}) async-start(), calls=%async_computation.6 | async-start | bytes 23654400 | tf_op jit(solution)/shard_map/all_gather | solution.py:35
  15.1 299.1 %all-gather.21.cloned.1.call-start = ((), (), s32[]{:S(2)}) async-start(), calls=%async_computation.8 | async-start | bytes 23654400 | tf_op jit(solution)/shard_map/all_gather | solution.py:35
  15.6 360.4 %all-gather.23.cloned.1.call-start = ((), (), s32[]{:S(2)}) async-start(), calls=%async_computation.9 | async-start | bytes 11827200 | tf_op jit(solution)/shard_map/all_gather | solution.py:35
  16.2 421.8 %all-gather.19.cloned.1.call-start = ((), (), s32[]{:S(2)}) async-start(), calls=%async_computation.7 | async-start | bytes 11827200 | tf_op jit(solution)/shard_map/all_gather | solution.py:35
  16.8 976.6 %reduce-scatter.21.cloned.1.call-start = ((), (), s32[]{:S(2)}) async-start(), calls=%async_computation.12 | async-start | bytes 11827200
  28.4 108.1 %copy-start.13 = (f32[2048]{0:T(1024)}, f32[2048]{0:T(1024)S(1)}, u32[]{:S(2)}) copy-start(f32[2048]{0:T(1024)S(1)} %add_rsqrt_fusion) | copy-start | bytes 24580
  271.9 75.4 %copy-start.11 = (f32[2048]{0:T(1024)}, f32[2048]{0:T(1024)S(1)}, u32[]{:S(2)}) copy-start(f32[2048]{0:T(1024)S(1)} %get-tuple-element.63) | copy-start | bytes 24580
  528.0 34.2 %copy-start.12 = (f32[2048]{0:T(1024)S(1)}, f32[2048]{0:T(1024)}, u32[]{:S(2)}) copy-start(f32[2048]{0:T(1024)} %copy-done.11) | copy-start | bytes 24580
  574.6 33.0 %copy-start.14 = (f32[2048]{0:T(1024)S(1)}, f32[2048]{0:T(1024)}, u32[]{:S(2)}) copy-start(f32[2048]{0:T(1024)} %copy-done.13) | copy-start | bytes 24580
  645.0 356.8 %reduce-scatter.23.cloned.1.call-start = ((), (), s32[]{:S(2)}) async-start(), calls=%async_computation.13 | async-start | bytes 11827200
  682.8 438.5 %reduce-scatter.17.cloned.1.call-start = ((), (), s32[]{:S(2)}) async-start(), calls=%async_computation.10 | async-start | bytes 11827200
  727.5 513.0 %reduce-scatter.19.cloned.1.call-start = ((), (), s32[]{:S(2)}) async-start(), calls=%async_computation.11 | async-start | bytes 11827200
  758.8 545.6 %all-reduce.12.cloned.1.call-start = ((), (), s32[]{:S(2)}) async-start(), calls=%async_computation.14 | async-start | bytes 4341760 | tf_op jit(solution)/shard_map/psum | solution.py:38
  827.3 152.6 %copy-start.15 = (u32[128]{0:T(128)S(1)}, u32[128]{0:T(128)}, u32[]{:S(2)}) copy-start(u32[128]{0:T(128)} %constant.51) | copy-start | bytes 1540
  827.3 477.1 %copy-start = (bf16[2,140,1280]{2,0,1:T(2,128)(2,1)S(1)}, bf16[2,140,1280]{2,0,1:T(2,128)(2,1)}, u32[]{:S(2)}) copy-start(bf16[2,140,1280]{2,0,1:T(2,128)(2,1)} %param.15) | copy-start | bytes 2150404
  973.5 8.4 collective-permute-start
  978.0 7.4 collective-permute-start.1
  983.4 329.9 %copy-start.1 = (bf16[2,40,4480]{2,1,0:T(8,128)(2,1)S(1)}, bf16[2,40,4480]{2,1,0:T(8,128)(2,1)}, u32[]{:S(2)}) copy-start(bf16[2,40,4480]{2,1,0:T(8,128)(2,1)} %param.13) | copy-start | bytes 2150404
  983.4 329.9 %copy-start.2 = (bf16[2,40,4480]{2,1,0:T(8,128)(2,1)S(1)}, bf16[2,40,4480]{2,1,0:T(8,128)(2,1)}, u32[]{:S(2)}) copy-start(bf16[2,40,4480]{2,1,0:T(8,128)(2,1)} %param.14) | copy-start | bytes 2150404
  1304.4 8.9 copy-start.3
  1304.4 8.9 copy-start.4
  1304.4 8.9 copy-start.5
  1304.4 8.9 copy-start.6
  1304.4 8.9 copy-start.7
  1304.4 8.9 copy-start.8
  1304.4 8.9 copy-start.9
  1304.4 8.9 copy-start.10
Sparse Core Ops, SparseCore 0:
  10.8 63.4 all-gather.12
  77.1 59.2 all-gather.14
  139.3 86.0 all-gather.16
  228.2 85.9 all-gather.20
  316.9 59.1 all-gather.22
  378.7 59.2 all-gather.18
  645.1 113.6 reduce-scatter.20
  762.7 239.0 reduce-scatter.22
  1005.6 115.5 reduce-scatter.16
  1124.9 115.5 reduce-scatter.18
  1243.8 60.5 all-reduce.11
where the time goes:
time: 1330 us; the launch traced here: 1320 us
  matrix products  566 us (43%)
  waiting for transfers between devices  528 us (40%)
  blocking collectives  146 us (11%)
  local copies, waits for them, and re-layouts  39.7 us (3%)
  other arithmetic  22.6 us (2%)
  between operations  15.2 us (1%)
    unnamed x17, waiting for transfers between devices  252 us
    all_gather x6, waiting for transfers between devices, fetched(): lax.all_gather(w[number], 's', axis=0, tiled=True)  213 us
    dot_general x5, matrix products, layer(): gate = jnp.dot(a, w['w_gate'], preferred_element_type=jnp.float32)  197 us
    dot_general x5, matrix products, layer(): up = jnp.dot(a, w['w_up'], preferred_element_type=jnp.float32)  188 us
    dot_general x5, matrix products, matmul(): jnp.dot(a, w, preferred_element_type=jnp.float32).astype(jnp.bfloat16)  181 us
    unnamed x1, blocking collectives  146 us
    psum x1, waiting for transfers between devices, summed(): lax.psum(lax.psum_scatter(term, 's', scatter_dimension=0, tiled=True), 'r')  63.9 us
    unnamed x42, local copies, waits for them, and re-layouts  29.3 us
  transfers between devices with their start and end apart: 13, of which 12 were waited for; matrix products, arithmetic and copies ran while one was open for 42% of the time, Pallas kernels for 0%

commit v1 on v0

v1 whole, which is shorter than its diff:
```python
import functools

import jax
import jax.numpy as jnp
from jax import lax
from jax.experimental import pallas as pl
from jax.experimental.pallas import tpu as pltpu
from jax.sharding import PartitionSpec as P

NAMES = ("w_gate", "w_up", "w_down")
MESH = pl.DeviceIdType.MESH
F32, BF16 = jnp.float32, jnp.bfloat16


def matmul(a, w):
    return jnp.dot(a, w, preferred_element_type=jnp.float32).astype(jnp.bfloat16)


def normed(h):
    wide = h.astype(jnp.float32)
    scale = lax.rsqrt(jnp.mean(wide**2, -1, keepdims=True) + 1e-6)
    return (wide * scale).astype(jnp.bfloat16)


def adamw(w, m, v, g):
    m = 0.9 * m + 0.1 * g
    v = 0.95 * v + 0.05 * g * g
    step = m * lax.rsqrt(v + 1e-8) + 0.1 * w
    return (w - 0.02 * step).astype(jnp.bfloat16), m, v


WIDE, TALL = "wide", "tall"
QUARTER = {WIDE: (40, 1152), TALL: (72, 640)}


def quarter_of(kind, grad, y, z, c, q):
    if kind == WIDE:
        return grad.at[y, z, pl.ds(pl.multiple_of(40 * c, 8), 40), pl.ds(1152 * q, 1152 if q < 3 else 1024)]
    return grad.at[y, z, pl.ds(72 * q, 72 if q < 3 else 64), pl.ds(pl.multiple_of(640 * c, 128), 640)]


def filled(kind, buffer, q):
    if q < 3:
        return buffer
    return buffer.at[:, :, pl.ds(0, 1024)] if kind == WIDE else buffer.at[:, pl.ds(0, 64), :]


def place():
    s = lax.axis_index("s")
    return lax.axis_index("r"), s // 8, (s // 2) % 4, s % 2


def chip(y, z, c):
    return {"s": (y * 4 + z) * 2 + c}


def turned(u, by):
    return (u + by) % 4


def remote(src, dst, sems, k, where):
    return pltpu.make_async_remote_copy(
        src_ref=src, dst_ref=dst, send_sem=sems[0].at[k], recv_sem=sems[1].at[k], device_id=where, device_id_type=MESH
    )


def added(*terms):
    total = terms[0].astype(F32)
    for term in terms[1:]:
        total = total + term.astype(F32)
    return total.astype(BF16)


def greet():
    x, y, z, c = place()
    others = [chip(y, z, 1 - c), chip(turned(y, 1), z, c), chip(turned(y, 3), z, c), chip(y, turned(z, 1), c), chip(y, turned(z, 3), c)]
    others += [{"r": turned(x, by)} for by in (1, 2, 3)]
    barrier = pltpu.get_barrier_semaphore()
    for other in others:
        pl.semaphore_signal(barrier, inc=1, device_id=other, device_id_type=MESH)
    pl.semaphore_wait(barrier, len(others))


class First:
    ORDER = (2, 1, 3, 0)

    def __init__(self, kind):
        self.kind, (rows, cols) = kind, QUARTER[kind]
        self.scratch = [
            pltpu.VMEM((4, 4, 4, rows, cols), BF16),
            pltpu.VMEM((4, 4, 4, rows, cols), BF16),
            pltpu.VMEM((2, 2, 4, rows, cols), BF16),
            pltpu.VMEM((2, 2, 2, 4, rows, cols), BF16),
            pltpu.SemaphoreType.DMA((16,)),
            pltpu.SemaphoreType.DMA((16,)),
            pltpu.SemaphoreType.DMA((16,)),
            pltpu.SemaphoreType.DMA((4,)),
            pltpu.SemaphoreType.DMA((4,)),
            pltpu.SemaphoreType.DMA((8,)),
            pltpu.SemaphoreType.DMA((8,)),
        ]
        self.out = jax.ShapeDtypeStruct((2, 2, 4, rows, cols), BF16)

    def bind(self, grad, out, refs):
        self.grad, self.out_ref = grad, out
        self.sums, self.theirs, self.near, self.far, self.load, *sems = refs
        self.swap, self.one, self.two = sems[0:2], sems[2:4], sems[4:6]

    def copies0(self, turn, p, j, c, mine):
        _, y, z, _ = place()
        k, q = (turn * 2 + p) * 2 + j, 2 * p + j
        at = turned(y if p == 0 else z, turn)
        part = quarter_of(self.kind, self.grad, *((at, slice(None)) if p == 0 else (slice(None), at)), c, q)
        into = filled(self.kind, (self.sums if mine else self.theirs).at[q, at], q)
        if mine:
            return pltpu.make_async_copy(part, into, self.load.at[k])
        return remote(part, into, self.swap, k, chip(y, z, 1 - place()[3]))

    def neighbours(self, p):
        _, y, z, c = place()
        if p == 0:
            return y, (chip(turned(y, 1), z, c), chip(turned(y, 3), z, c))
        return z, (chip(y, turned(z, 1), c), chip(y, turned(z, 3), c))

    def copy1(self, p, d):
        u, to = self.neighbours(p)
        return remote(self.sums.at[2 * p + d, turned(u, 2)], self.near.at[p, d], self.one, 2 * p + d, to[d])

    def copy2(self, p, d, j):
        u, to = self.neighbours(p)
        return remote(self.sums.at[2 * p + j, turned(u, (1, 3)[d])], self.far.at[p, d, j], self.two, 4 * p + 2 * d + j, to[d])

    def start(self):
        c = place()[3]
        for turn in self.ORDER:
            for p in range(2):
                for j in range(2):
                    self.copies0(turn, p, j, 1 - c, False).start()
                    self.copies0(turn, p, j, c, True).start()

    def pair(self, *turns):
        c = place()[3]
        for turn in turns:
            for p in range(2):
                for j in range(2):
                    self.copies0(turn, p, j, c, True).wait()
                    self.copies0(turn, p, j, 1 - c, False).wait_recv()
        for turn in turns:
            for p in range(2):
                at = turned(self.neighbours(p)[0], turn)

                def one(i, _, p=p, at=at):
                    for j in range(2):
                        q = 2 * p + j
                        self.sums[q, at, i] = added(self.sums[q, at, i], self.theirs[q, at, i])
                    return 0

                lax.fori_loop(0, 4, one, 0)

    def send1(self):
        for p in range(2):
            for d in range(2):
                self.copy1(p, d).start()

    def send2(self):
        for p in range(2):
            for d in range(2):
                self.copy1(p, d).wait_recv()
        for p in range(2):
            u = self.neighbours(p)[0]

            def one(i, _, p=p, u=u):
                for d in range(2):
                    at = turned(u, (1, 3)[d])
                    self.sums[2 * p + d, at, i] = added(self.sums[2 * p + d, at, i], self.near[p, d, i])
                return 0

            lax.fori_loop(0, 4, one, 0)
        for p in range(2):
            for d in range(2):
                for j in range(2):
                    self.copy2(p, d, j).start()

    def finish(self):
        for p in range(2):
            for d in range(2):
                for j in range(2):
                    self.copy2(p, d, j).wait_recv()
        for p in range(2):
            u = self.neighbours(p)[0]

            def one(i, _, p=p, u=u):
                for j in range(2):
                    self.out_ref[p, j, i] = added(self.sums[2 * p + j, u, i], self.far[p, 0, j, i], self.far[p, 1, j, i])
                return 0

            lax.fori_loop(0, 4, one, 0)
        c = place()[3]
        for p in range(2):
            for d in range(2):
                self.copy1(p, d).wait_send()
                for j in range(2):
                    self.copy2(p, d, j).wait_send()
        for turn in self.ORDER:
            for p in range(2):
                for j in range(2):
                    self.copies0(turn, p, j, 1 - c, False).wait_send()

    def slots(self):
        return {0: [self.start], 2: [functools.partial(self.pair, 2), self.send1], 4: [functools.partial(self.pair, 1, 3)], 5: [functools.partial(self.pair, 0)], 7: [self.send2], 99: [self.finish]}


class Second:
    def __init__(self, kind):
        rows, cols = QUARTER[kind]
        self.part = jax.ShapeDtypeStruct((2, 2, 4, rows, cols), BF16)
        self.out = jax.ShapeDtypeStruct((4, rows, cols), BF16)
        self.scratch = [
            pltpu.VMEM((2, 2, rows, cols), BF16),
            pltpu.VMEM((2, 2, 2, rows, cols), BF16),
            pltpu.VMEM((2, 2, 2, rows, cols), BF16),
            pltpu.VMEM((4, rows, cols), BF16),
            pltpu.VMEM((4, rows, cols), BF16),
            pltpu.VMEM((4, rows, cols), BF16),
            pltpu.SemaphoreType.DMA((4,)),
            pltpu.SemaphoreType.DMA((4,)),
            pltpu.SemaphoreType.DMA((4,)),
            pltpu.SemaphoreType.DMA((4,)),
            pltpu.SemaphoreType.DMA((3,)),
            pltpu.SemaphoreType.DMA((3,)),
            pltpu.SemaphoreType.DMA((3,)),
            pltpu.SemaphoreType.DMA((3,)),
        ]

    def bind(self, part, out, refs):
        self.part_ref, self.out_ref = part, out
        self.near, self.far, self.onward, self.block, self.copies, self.whole, *sems = refs
        self.one, self.two, self.cut, self.join = sems[0:2], sems[2:4], sems[4:6], sems[6:8]

    def neighbours(self, p):
        _, y, z, c = place()
        if p == 1:
            return y, (chip(turned(y, 1), z, c), chip(turned(y, 3), z, c))
        return z, (chip(y, turned(z, 1), c), chip(y, turned(z, 3), c))

    def copy1(self, p, d):
        u, to = self.neighbours(p)
        return remote(self.part_ref.at[p, d, turned(u, 2)], self.near.at[p, d], self.one, 2 * p + d, to[d])

    def copy2(self, p, d):
        return remote(self.onward.at[p, d], self.far.at[p, d], self.two, 2 * p + d, self.neighbours(p)[1][d])

    def copy3(self, by):
        x = place()[0]
        return remote(self.block.at[turned(x, by)], self.copies.at[x], self.cut, by - 1, {"r": turned(x, by)})

    def copy4(self, by):
        x = place()[0]
        return remote(self.whole.at[x], self.whole.at[x], self.join, by - 1, {"r": turned(x, by)})

    def start(self):
        for p in range(2):
            for d in range(2):
                self.copy1(p, d).start()

    def send2(self):
        for p in range(2):
            for d in range(2):
                self.copy1(p, d).wait_recv()
        for p in range(2):
            u = self.neighbours(p)[0]
            for d in range(2):
                at = turned(u, (1, 3)[d])
                self.onward[p, d, d] = added(self.part_ref[p, d, at], self.near[p, d])
                self.onward[p, d, 1 - d] = self.part_ref[p, 1 - d, at]
        for p in range(2):
            for d in range(2):
                self.copy2(p, d).start()

    def send3(self):
        for p in range(2):
            for d in range(2):
                self.copy2(p, d).wait_recv()
        for p in range(2):
            u = self.neighbours(p)[0]
            for j in range(2):
                self.block[2 * p + j] = added(self.part_ref[p, j, u], self.far[p, 0, j], self.far[p, 1, j])
        for by in (1, 2, 3):
            self.copy3(by).start()
        x = place()[0]
        self.copies[x] = self.block[x]

    def send4(self):
        for by in (1, 2, 3):
            self.copy3(by).wait_recv()
        x = place()[0]
        self.whole[x] = added(*(self.copies[i] for i in range(4)))
        for by in (1, 2, 3):
            self.copy4(by).start()

    def finish(self):
        for by in (1, 2, 3):
            self.copy4(by).wait_recv()
        self.out_ref[...] = self.whole[...]
        for p in range(2):
            for d in range(2):
                self.copy1(p, d).wait_send()
                self.copy2(p, d).wait_send()
        for by in (1, 2, 3):
            self.copy3(by).wait_send()
            self.copy4(by).wait_send()

    def slots(self):
        return {0: [self.start], 2: [self.send2], 5: [self.send3], 9: [self.send4], 12: [self.finish]}


TILE = 640


def travel(name, number, first, grad, second, part, product=None):
    jobs, inputs, in_specs, outs, out_specs, scratch = [], [], [], [], [], []
    whole = lambda shape: pl.BlockSpec(shape, lambda *_: (0,) * len(shape))
    grid, steps, extra = (1,), 1, {}
    if product is not None:
        lhs, rhs = product
        tall = lhs.shape[1] > rhs.shape[1]
        grid, steps = (7, 2), 14
        depth = lhs.shape[0]
        moving = pl.BlockSpec((depth, TILE), lambda i, j: (0, i))
        still = pl.BlockSpec((depth, 2 * TILE), lambda i, j: (0, 0))
        inputs += [lhs, rhs]
        in_specs += [moving, still] if tall else [still, moving]
        outs.append(jax.ShapeDtypeStruct((lhs.shape[1], rhs.shape[1]), BF16))
        out_specs.append(pl.BlockSpec((TILE, TILE), (lambda i, j: (i, j)) if tall else (lambda i, j: (j, i))))
        extra = dict(
            cost_estimate=pl.CostEstimate(
                flops=2 * depth * lhs.shape[1] * rhs.shape[1], bytes_accessed=60_000_000, transcendentals=0
            )
        )
    if first is not None:
        jobs.append((First(first), grad))
    if second is not None:
        jobs.append((Second(second), part))
    for job, source in jobs:
        inputs.append(source)
        in_specs.append(pl.BlockSpec(memory_space=pl.ANY) if isinstance(job, First) else whole(job.part.shape))
        outs.append(job.out)
        out_specs.append(whole(job.out.shape))
        scratch += job.scratch

    def body(*refs):
        n_in, n_out = len(inputs), len(outs)
        ins, results, rest = refs[:n_in], refs[n_in : n_in + n_out], list(refs[n_in + n_out :])
        skip = 0 if product is None else 2
        plan = {}
        for k, (job, _) in enumerate(jobs):
            job.bind(ins[skip + k], results[(0 if product is None else 1) + k], rest[: len(job.scratch)])
            rest = rest[len(job.scratch) :]
            for slot, actions in job.slots().items():
                plan.setdefault(slot, []).extend(actions)

        def act(slot):
            if slot == 0:
                greet()
            for action in plan.get(slot, []):
                action()

        if product is None:
            for slot in sorted(plan):
                act(slot)
            return
        i, j = pl.program_id(0), pl.program_id(1)
        now = i * 2 + j
        for slot in sorted(plan):
            if slot < steps:
                pl.when(now == slot)(functools.partial(act, slot))
        lhs_ref, rhs_ref = ins[:2]
        piece = pl.ds(pl.multiple_of(j * TILE, 128), TILE)
        left, right = (lhs_ref[...], rhs_ref[:, piece]) if tall else (lhs_ref[:, piece], rhs_ref[...])
        results[0][...] = lax.dot_general(left, right, (((0,), (0,)), ((), ())), preferred_element_type=F32).astype(BF16)

        @pl.when(now == steps - 1)
        def _():
            for slot in sorted(plan):
                if slot >= steps:
                    act(slot)

    return pl.pallas_call(
        body,
        out_shape=tuple(outs),
        grid=grid,
        in_specs=in_specs,
        out_specs=tuple(out_specs),
        scratch_shapes=scratch,
        name=name,
        compiler_params=pltpu.CompilerParams(
            collective_id=number,
            has_side_effects=True,
            vmem_limit_bytes=61_000_000,
            dimension_semantics=("arbitrary",) * len(grid),
        ),
        **extra,
    )(*inputs)


def blocks(grad):
    return grad.reshape(4, 4, grad.shape[0] // 16, grad.shape[1])


def wide_gradient(out):
    return jnp.transpose(out, (1, 0, 2)).reshape(40, 4608)[:, :4480]


def tall_gradient(out):
    half = out.reshape(288, 640)[:280]
    other = lax.ppermute(half, "s", [(i, i ^ 1) for i in range(32)])
    c = lax.axis_index("s") % 2
    both = jnp.where(c == 0, jnp.concatenate([half, other], 1), jnp.concatenate([other, half], 1))
    return lax.dynamic_slice(both, (140 * c, 0), (140, 1280))


def solution(mesh):
    def fetched(w, number, name):
        if name == "w_down":
            padded = jnp.pad(w[number], ((0, 4), (0, 0)))
            return lax.all_gather(padded, "s", axis=0)[:, :140].reshape(4480, 1280)
        return lax.all_gather(w[number], "s", axis=0, tiled=True)

    def step(x, dy, *arrays):
        weights, m, v = (arrays[i : i + 3] for i in (0, 3, 6))
        full = [{name: fetched(w, number, name) for name, w in zip(NAMES, weights, strict=True)} for number in range(2)]

        def up_to_hidden(a, w):
            gate = jnp.dot(a, w["w_gate"], preferred_element_type=F32)
            up = jnp.dot(a, w["w_up"], preferred_element_type=F32)
            return (jax.nn.silu(gate) * up).astype(BF16), (gate, up)

        def split(gate, up, by_hidden):
            _, back = jax.vjp(lambda gate, up: (jax.nn.silu(gate) * up).astype(BF16), gate, up)
            by_gate, by_up = back(by_hidden)
            return by_gate.astype(BF16), by_up.astype(BF16)

        h0, by_y = x[0], dy[0]
        a0 = normed(h0)
        hid0, pre0 = up_to_hidden(a0, full[0])
        h1 = h0 + matmul(hid0, full[0]["w_down"])
        a1, back_norm = jax.vjp(normed, h1)
        hid1, pre1 = up_to_hidden(a1, full[1])

        transposed = lambda g, w: lax.dot_general(g, w, (((1,), (1,)), ((), ())), preferred_element_type=F32)
        by_hid1 = transposed(by_y, full[1]["w_down"]).astype(BF16)
        by_gate1, by_up1 = split(*pre1, by_hid1)
        d1 = lax.dot_general(hid1, by_y, (((0,), (0,)), ((), ())), preferred_element_type=F32).astype(BF16)
        g1, part_d1 = travel("g1", 1, TALL, blocks(d1), None, None, (a1, by_gate1))
        u1, part_g1, sum_d1 = travel("u1", 2, WIDE, blocks(g1), TALL, part_d1, (a1, by_up1))
        by_a1 = transposed(by_gate1, full[1]["w_gate"]).astype(BF16) + transposed(by_up1, full[1]["w_up"]).astype(BF16)
        by_h1 = by_y + back_norm(by_a1)[0]
        by_hid0 = transposed(by_h1, full[0]["w_down"]).astype(BF16)
        by_gate0, by_up0 = split(*pre0, by_hid0)
        d0, part_u1, sum_g1 = travel("d0", 3, WIDE, blocks(u1), WIDE, part_g1, (hid0, by_h1))
        g0, part_d0, sum_u1 = travel("g0", 4, TALL, blocks(d0), WIDE, part_u1, (a0, by_gate0))
        u0, part_g0, sum_d0 = travel("u0", 5, WIDE, blocks(g0), TALL, part_d0, (a0, by_up0))
        part_u0, sum_g0 = travel("t0", 6, WIDE, blocks(u0), WIDE, part_g0)
        (sum_u0,) = travel("t1", 7, None, None, WIDE, part_u0)
        gradients = [
            jnp.stack([wide_gradient(sum_g0), wide_gradient(sum_g1)]),
            jnp.stack([wide_gradient(sum_u0), wide_gradient(sum_u1)]),
            jnp.stack([tall_gradient(sum_d0), tall_gradient(sum_d1)]),
        ]
        new = [adamw(w.astype(F32), m, v, g.astype(F32)) for w, m, v, g in zip(weights, m, v, gradients, strict=True)]
        return tuple(one[which] for which in range(3) for one in new)

    states, cut = P(("rep", "r", "s"), None, None), P(None, "s", None)
    return jax.shard_map(
        step,
        mesh=mesh,
        in_specs=(states, states) + (cut,) * 9,
        out_specs=(P("rep", "s", None),) * 9,
        check_vma=False,
    )
```

time: 1330 us -> 947 us (0.71)
  waiting for transfers between devices: 528 us -> 159 us
  Pallas kernels: 0 us -> 306 us
  matrix products: 566 us -> 381 us
  blocking collectives: 146 us -> 0 us
    pallas_call x0 -> x7, Pallas kernels: none -> 306 us  [travel(): pl.pallas_call(body, out_shape=tuple(outs), grid=grid, in_specs=in_specs,...]
    unnamed x17 -> x6, waiting for transfers between devices: 252 us -> 1.12 us
    dot_general x5 -> x1, matrix products: 181 us -> 31.9 us  [matmul(): jnp.dot(a, w, preferred_element_type=jnp.float32).astype(jnp.bfloat16)]
    unnamed x1 -> x0, blocking collectives: 146 us -> none
    psum x1 -> x0, waiting for transfers between devices: 63.9 us -> none  [summed(): lax.psum(lax.psum_scatter(term, 's', scatter_dimension=0, tiled=True), 'r')]
    all_gather x6, waiting for transfers between devices: 213 us -> 158 us  [the longest x4 92.2 us: fetched(): return lax.all_gather(w[number], 's', axis=0, tiled=True)]
    dot_general x10 -> x9, matrix products: 384 us -> 349 us  [the longest x4 145 us: step(): lax.dot_general(g, w, (((1,), (1,)), ((), ())), preferred_element_type=F32)]
    reshape x0 -> x6, local copies, waits for them, and re-layouts: none -> 33 us  [the longest x2 28.7 us: fetched(): return lax.all_gather(padded, 's', axis=0)[:, :140].reshape(4480, 1280)]
  transfers between devices with their start and end apart: 13 -> 8, of which waited for: 12 -> 5; matrix products, arithmetic and copies ran while one was open for 42% -> 23% of each run, Pallas kernels for 0% -> 0%
where the time goes in v1:
time: 947 us; the launch traced here: 943 us
  matrix products  381 us (40%)
  Pallas kernels  306 us (32%)
  waiting for transfers between devices  159 us (17%)
  local copies, waits for them, and re-layouts  50.1 us (5%)
  other arithmetic  26.5 us (3%)
  between operations  14.7 us (2%)
    pallas_call x7, Pallas kernels, travel(): pl.pallas_call(body, out_shape=tuple(outs), grid=grid, in_specs=in_specs,...  306 us
    dot_general x4, matrix products, step(): lax.dot_general(g, w, (((1,), (1,)), ((), ())), preferred_element_type=F32)  145 us
    all_gather x4, waiting for transfers between devices, fetched(): return lax.all_gather(w[number], 's', axis=0, tiled=True)  92.2 us
    dot_general x2, matrix products, up_to_hidden(): gate = jnp.dot(a, w['w_gate'], preferred_element_type=F32)  88.7 us
    dot_general x2, matrix products, up_to_hidden(): up = jnp.dot(a, w['w_up'], preferred_element_type=F32)  77.4 us
    all_gather x2, waiting for transfers between devices, fetched(): return lax.all_gather(padded, 's', axis=0)[:, :140].reshape(4480, 1280)  65.7 us
    dot_general x1, matrix products, step(): lax.dot_general(hid1, by_y, (((0,), (0,)), ((), ())), preferred_element_t...  38.4 us
    dot_general x1, matrix products, matmul(): jnp.dot(a, w, preferred_element_type=jnp.float32).astype(jnp.bfloat16)  31.9 us
  transfers between devices with their start and end apart: 8, of which 5 were waited for; matrix products, arithmetic and copies ran while one was open for 23% of the time, Pallas kernels for 0%

profile of v1, /device:TPU:1, one launch (start us, length us, event | category | flops | bytes accessed | tf_op | source)
XLA Modules:
  0.0 943.1 jit_solution(3012443941197494749)
XLA Ops:
  7.2 0.0 all-gather.13.cloned.1.call-start
  7.2 2.0 fusion.75
  9.2 0.0 all-gather.17.cloned.1.call-start
  9.3 2.0 fusion.74
  11.3 0.0 all-gather.17.cloned.1.call-update
  11.3 0.0 all-gather.19.cloned.1.call-start
  11.4 1.2 copy.24
  12.6 0.1 slice_bitcast_fusion.1
  12.6 0.8 pad.8
  13.4 0.0 all-gather.15.cloned.1.call-start
  13.4 0.8 pad.7
  14.2 0.0 all-gather.21.cloned.1.call-start
  14.3 0.5 all-gather.21.cloned.1.call-update
  14.8 0.0 all-gather.23.cloned.1.call-start
  14.9 0.5 all-gather.23.cloned.1.call-update
  15.4 3.6 fusion.22
  19.0 5.7 fusion.23.refs_0_
  24.7 49.6 %all-gather.13.cloned.1.call-done = bf16[1,1280,4480]{2,1,0:T(8,128)(2,1)} async-done(((bf16[1,40,4480]{2,1,0:T(8,128)(2,1)}), bf16[1,1280,4480]{2,1,0:T(8,128)(2,1)}) %all-gather.13.cloned.1.call-update) | async-done | bytes 11468816 | tf_op jit(solution)/shard_map/all_gather | solution.py:427
  74.3 31.5 %fusion.20 = f32[2048,4480]{1,0:T(8,128)} fusion(bf16[2048,1280]{1,0:T(8,128)(2,1)} %fusion.23.refs_0_, bf16[1,1280,4480]{2,1,0:T(8,128)(2,1)} %all-gather.13.cloned.1.call-done), kind=kOutput, calls=%fused_computation.40 | convolution fusion | flops 23488102400 | bytes 53411840 | tf_op jit(solution)/shard_map/dot_general | solution.py:434
  105.8 30.6 %all-gather.17.cloned.1.call-done = bf16[1,1280,4480]{2,1,0:T(8,128)(2,1)} async-done(((bf16[1,40,4480]{2,1,0:T(8,128)(2,1)}), bf16[1,1280,4480]{2,1,0:T(8,128)(2,1)}) %all-gather.17.cloned.1.call-update) | async-done | bytes 11468816 | tf_op jit(solution)/shard_map/all_gather | solution.py:427
  136.4 45.7 %multiply_convert_fusion.1 = (bf16[2048,4480]{1,0:T(8,128)(2,1)}, f32[2048,4480]{1,0:T(8,128)}) fusion(f32[2048,4480]{1,0:T(8,128)} %fusion.20, bf16[2048,1280]{1,0:T(8,128)(2,1)} %fusion.23.refs_0_, bf16[1,1280,4480]{2,1,0:T(8,128)(2,1)} %all-gather.17.cloned.1.call-done), kind=kOutput, calls=%fused_computation.17 | convolution fusion | flops 23543152640 | bytes 108462080 | tf_op jit(solution)/shard_map/dot_general | solution.py:435
  182.2 17.2 %all-gather.19.cloned.1.call-done = bf16[4608,1280]{1,0:T(8,128)(2,1)} async-done(((bf16[144,1280]{1,0:T(8,128)(2,1)}), bf16[4608,1280]{1,0:T(8,128)(2,1)}) %all-gather.19.cloned.1.call-update) | async-done | bytes 11796496 | tf_op jit(solution)/shard_map/all_gather | solution.py:426
  199.4 14.3 %reshape.85 = bf16[4480,1280]{1,0:T(8,128)(2,1)} reshape(bf16[32,140,1280]{2,1,0:T(8,128)(2,1)} %bitcast.96) | data formatting | bytes 22937600 | tf_op jit(solution)/shard_map/reshape | solution.py:426
  213.7 48.5 %all-gather.15.cloned.1.call-done = bf16[4608,1280]{1,0:T(8,128)(2,1)} async-done(((bf16[144,1280]{1,0:T(8,128)(2,1)}), bf16[4608,1280]{1,0:T(8,128)(2,1)}) %all-gather.15.cloned.1.call-update) | async-done | bytes 11796496 | tf_op jit(solution)/shard_map/all_gather | solution.py:426
  262.2 14.4 %reshape.84 = bf16[4480,1280]{1,0:T(8,128)(2,1)} reshape(bf16[32,140,1280]{2,1,0:T(8,128)(2,1)} %bitcast.97) | data formatting | bytes 22937600 | tf_op jit(solution)/shard_map/reshape | solution.py:426
  276.6 31.9 %fusion.26 = (f32[2048]{0:T(1024)S(1)}, bf16[2048,1280]{1,0:T(8,128)(2,1)S(1)}) fusion(bf16[2048,4480]{1,0:T(8,128)(2,1)} %get-tuple-element.69.refs_0_, bf16[4480,1280]{1,0:T(8,128)(2,1)} %reshape.85, bf16[1,2048,1280]{2,1,0:T(8,128)(2,1)} %param.11), kind=kOutput, calls=%fused_computation.46 | convolution fusion | flops 23501207552 | bytes 40312832 | tf_op jit(solution)/shard_map/dot_general | solution.py:16
  308.5 0.6 copy-done.13
  309.1 1.7 copy-done
  310.7 0.1 copy-done.11
  310.8 3.2 fusion.27.refs_0_
  314.0 28.6 %convolution_convert_fusion.2 = bf16[4480,2048]{0,1:T(8,128)(2,1)} fusion(bf16[4480,1280]{1,0:T(8,128)(2,1)S(1)} %bitcast.100, bf16[1,2048,1280]{2,1,0:T(8,128)(2,1)} %param.12), kind=kOutput, calls=%fused_computation.22 | convolution fusion | flops 23497277440 | bytes 35061760 | tf_op jit(solution)/shard_map/dot_general | solution.py:450
  342.6 31.7 %fusion.16 = f32[2048,4480]{1,0:T(8,128)} fusion(bf16[2048,1280]{1,0:T(8,128)(2,1)} %fusion.27.refs_0_, bf16[1,1280,4480]{2,1,0:T(8,128)(2,1)} %all-gather.21.cloned.1.call-done), kind=kOutput, calls=%fused_computation.36 | convolution fusion | flops 23488102400 | bytes 53411840 | tf_op jit(solution)/shard_map/dot_general | solution.py:435
  374.3 11.9 %all-gather.23.cloned.1.call-done = bf16[1,1280,4480]{2,1,0:T(8,128)(2,1)} async-done(((bf16[1,40,4480]{2,1,0:T(8,128)(2,1)}), bf16[1,1280,4480]{2,1,0:T(8,128)(2,1)}) %all-gather.23.cloned.1.call-update) | async-done | bytes 11468816 | tf_op jit(solution)/shard_map/all_gather | solution.py:427
  386.2 57.2 %fusion.3 = (bf16[2048,4480]{1,0:T(8,128)(2,1)}, bf16[2048,4480]{1,0:T(8,128)(2,1)}, f32[2048,4480]{1,0:T(8,128)}) fusion(f32[2048,4480]{1,0:T(8,128)} %fusion.16, bf16[4480,2048]{0,1:T(8,128)(2,1)} %convolution_convert_fusion.2, bf16[2048,1280]{1,0:T(8,128)(2,1)} %fusion.27.refs_0_, bf16[1,1280,4480]{2,1,0:T(8,128)(2,1)} %all-gather.23.cloned.1.call-done), kind=kOutput, calls=%fused_computation.7 | convolution fusion | flops 23625728000 | bytes 145162240 | tf_op jit(solution)/shard_map/dot_general | solution.py:434
  443.4 31.9 %fusion.29 = bf16[2048,1280]{1,0:T(8,128)(2,1)} fusion(bf16[2048,4480]{1,0:T(8,128)(2,1)} %get-tuple-element.62.refs_1_, bf16[1,1280,4480]{2,1,0:T(8,128)(2,1)} %all-gather.21.cloned.1.call-done), kind=kOutput, calls=%fused_computation.50 | convolution fusion | flops 23490723840 | bytes 35061760 | tf_op jit(solution)/shard_map/dot_general | solution.py:450
  475.3 33.8 %fusion.28 = (f32[2048]{0:T(1024)S(1)}, bf16[2048,1280]{1,0:T(8,128)(2,1)}) fusion(bf16[2048,1280]{1,0:T(8,128)(2,1)} %copy-done, bf16[2048,1280]{1,0:T(8,128)(2,1)} %fusion.29, bf16[2048,4480]{1,0:T(8,128)(2,1)} %get-tuple-element.61.refs_1_, bf16[1,1280,4480]{2,1,0:T(8,128)(2,1)} %all-gather.23.cloned.1.call-done), kind=kOutput, calls=%fused_computation.48 | convolution fusion | flops 23503828992 | bytes 45555712 | tf_op jit(solution)/shard_map/dot_general | solution.py:450
  509.1 38.4 %convolution_convert_fusion.1 = bf16[4480,1280]{1,0:T(8,128)(2,1)} fusion(f32[2048,4480]{1,0:T(8,128)} %fusion.16, f32[2048,4480]{1,0:T(8,128)} %get-tuple-element.73, bf16[1,2048,1280]{2,1,0:T(8,128)(2,1)} %param.12), kind=kOutput, calls=%fused_computation.21 | convolution fusion | flops 23548887040 | bytes 90112000 | tf_op jit(solution)/shard_map/dot_general | solution.py:453
  547.5 46.5 %g1.1 = (bf16[1280,4480]{1,0:T(8,128)(2,1)}, bf16[2,2,4,72,640]{4,3,2,1,0:T(8,128)(2,1)}) custom-call(bf16[2048,1280]{1,0:T(8,128)(2,1)} %fusion.27.refs_0_, bf16[2048,4480]{1,0:T(8,128)(2,1)} %get-tuple-element.61.refs_1_, bf16[4,4,280,1280]{3,2,1,0:T(8,128)(2,1)} %bitcast.115), custom_call_target="tpu_custom_call" | custom-call | flops 23488102400 | bytes 60000000 | tf_op jit(solution)/shard_map/g1/pallas_call | solution.py:388
  594.0 8.5 fusion.40.refs_1_
  602.5 48.0 %u1_.1 = (bf16[1280,4480]{1,0:T(8,128)(2,1)}, bf16[2,2,4,40,1152]{4,3,2,1,0:T(8,128)(2,1)}, bf16[4,72,640]{2,1,0:T(8,128)(2,1)}) custom-call(bf16[2048,1280]{1,0:T(8,128)(2,1)} %fusion.27.refs_0_, bf16[2048,4480]{1,0:T(8,128)(2,1)} %get-tuple-element.62.refs_1_, bf16[4,4,80,4480]{3,2,1,0:T(8,128)(2,1)} %bitcast.112, ...), custom_call_target="tpu_custom_call" | custom-call | flops 23488102400 | bytes 60000000 | tf_op jit(solution)/shard_map/u1/pallas_call | solution.py:388
  650.5 48.8 %d0.1 = (bf16[4480,1280]{1,0:T(8,128)(2,1)}, bf16[2,2,4,40,1152]{4,3,2,1,0:T(8,128)(2,1)}, bf16[4,40,1152]{2,1,0:T(8,128)(2,1)}) custom-call(bf16[2048,4480]{1,0:T(8,128)(2,1)} %get-tuple-element.69.refs_0_, bf16[2048,1280]{1,0:T(8,128)(2,1)} %fusion.40.refs_1_, bf16[4,4,80,4480]{3,2,1,0:T(8,128)(2,1)} %bitcast.114, ...), custom_call_target="tpu_custom_call" | custom-call | flops 23488102400 | bytes 60000000 | tf_op jit(solution)/shard_map/d0/pallas_call | solution.py:388
  699.3 1.0 copy.45
  700.3 50.6 %fusion.6 = (bf16[2048,4480]{1,0:T(8,128)(2,1)}, bf16[2048,4480]{1,0:T(8,128)(2,1)}) fusion(f32[2048,4480]{1,0:T(8,128)} %fusion.20, f32[2048,4480]{1,0:T(8,128)} %get-tuple-element.70, bf16[2048,1280]{1,0:T(8,128)(2,1)} %fusion.40.refs_1_, bf16[4480,1280]{1,0:T(8,128)(2,1)} %reshape.85), kind=kOutput, calls=%fused_computation.10 | convolution fusion | flops 23634903040 | bytes 126812160 | tf_op jit(solution)/shard_map/dot_general | solution.py:450
  751.0 48.6 %g0.1 = (bf16[1280,4480]{1,0:T(8,128)(2,1)}, bf16[2,2,4,72,640]{4,3,2,1,0:T(8,128)(2,1)}, bf16[4,40,1152]{2,1,0:T(8,128)(2,1)}) custom-call(bf16[2048,1280]{1,0:T(8,128)(2,1)} %fusion.23.refs_0_, bf16[2048,4480]{1,0:T(8,128)(2,1)} %get-tuple-element.59.refs_1_, bf16[4,4,280,1280]{3,2,1,0:T(8,128)(2,1)} %bitcast.111, ...), custom_call_target="tpu_custom_call" | custom-call | flops 23488102400 | bytes 60000000 | tf_op jit(solution)/shard_map/g0/pallas_call | solution.py:388
  799.6 48.7 %u0.1 = (bf16[1280,4480]{1,0:T(8,128)(2,1)}, bf16[2,2,4,40,1152]{4,3,2,1,0:T(8,128)(2,1)}, bf16[4,72,640]{2,1,0:T(8,128)(2,1)}) custom-call(bf16[2048,1280]{1,0:T(8,128)(2,1)} %fusion.23.refs_0_, bf16[2048,4480]{1,0:T(8,128)(2,1)} %get-tuple-element.60.refs_1_, bf16[4,4,80,4480]{3,2,1,0:T(8,128)(2,1)} %bitcast.113, ...), custom_call_target="tpu_custom_call" | custom-call | flops 23488102400 | bytes 60000000 | tf_op jit(solution)/shard_map/u0/pallas_call | solution.py:388
  848.3 44.1 %t0.1 = (bf16[2,2,4,40,1152]{4,3,2,1,0:T(8,128)(2,1)}, bf16[4,40,1152]{2,1,0:T(8,128)(2,1)}) custom-call(bf16[4,4,80,4480]{3,2,1,0:T(8,128)(2,1)} %bitcast.98, bf16[2,2,4,40,1152]{4,3,2,1,0:T(8,128)(2,1)} %get-tuple-element.34.refs_1_), custom_call_target="tpu_custom_call" | custom-call | tf_op jit(solution)/shard_map/t0/pallas_call | solution.py:388
  892.4 1.1 copy.44
  893.5 1.0 copy.47
  894.5 21.6 %t1.1 = bf16[4,40,1152]{2,1,0:T(8,128)(2,1)} custom-call(bf16[2,2,4,40,1152]{4,3,2,1,0:T(8,128)(2,1)} %get-tuple-element.37.refs_0_), custom_call_target="tpu_custom_call" | custom-call | tf_op jit(solution)/shard_map/t1/pallas_call | solution.py:388
  916.1 1.2 copy.46
  917.3 1.0 slice.65
  918.3 4.7 collective-permute-start.1
  923.0 1.0 slice.64
  924.0 0.3 collective-permute-start
  924.4 0.1 slice_bitcast_fusion.4
  924.4 0.1 slice_bitcast_fusion.2
  924.5 2.2 fusion.50
  926.7 2.2 fusion.54
  928.9 0.2 fusion.60
  929.1 0.2 fusion.64
  929.4 0.8 fusion.45
  930.2 1.4 copy.37
  931.6 2.2 copy.38
  933.8 2.2 copy.39
  (43 shorter events, 0.2 us)
Async XLA Ops:
  7.2 67.1 %all-gather.13.cloned.1.call-start = ((), (), s32[]{:S(2)}) async-start(), calls=%async_computation | async-start | bytes 11827200 | tf_op jit(solution)/shard_map/all_gather | solution.py:427
  9.2 127.2 %all-gather.17.cloned.1.call-start = ((), (), s32[]{:S(2)}) async-start(), calls=%async_computation.2 | async-start | bytes 11827200 | tf_op jit(solution)/shard_map/all_gather | solution.py:427
  11.3 188.1 %all-gather.19.cloned.1.call-start = ((), (), s32[]{:S(2)}) async-start(), calls=%async_computation.3 | async-start | bytes 12165120 | tf_op jit(solution)/shard_map/all_gather | solution.py:426
  13.4 248.8 %all-gather.15.cloned.1.call-start = ((), (), s32[]{:S(2)}) async-start(), calls=%async_computation.1 | async-start | bytes 12165120 | tf_op jit(solution)/shard_map/all_gather | solution.py:426
  14.2 328.4 %all-gather.21.cloned.1.call-start = ((), (), s32[]{:S(2)}) async-start(), calls=%async_computation.4 | async-start | bytes 11827200 | tf_op jit(solution)/shard_map/all_gather | solution.py:427
  14.8 371.4 %all-gather.23.cloned.1.call-start = ((), (), s32[]{:S(2)}) async-start(), calls=%async_computation.5 | async-start | bytes 11827200 | tf_op jit(solution)/shard_map/all_gather | solution.py:427
  276.5 37.4 %slice-start = ((s8[11468800]{0:T(1024)(128)(4,1)}), s8[4194304]{0:T(1024)(128)(4,1)S(1)}, s32[]{:S(2)}) async-start(s8[11468800]{0:T(1024)(128)(4,1)} %bitcast.99), calls=%async_computation.6 | async-start | bytes 8388608
  276.5 37.4 %slice-start.1 = ((s8[11468800]{0:T(1024)(128)(4,1)}), s8[4194304]{0:T(1024)(128)(4,1)S(1)}, s32[]{:S(2)}) async-start(s8[11468800]{0:T(1024)(128)(4,1)} %bitcast.99), calls=%async_computation.7 | async-start | bytes 8388608
  276.5 37.4 %slice-start.2 = ((s8[11468800]{0:T(1024)(128)(4,1)}), s8[3080192]{0:T(1024)(128)(4,1)S(1)}, s32[]{:S(2)}) async-start(s8[11468800]{0:T(1024)(128)(4,1)} %bitcast.99), calls=%async_computation.8 | async-start | bytes 6160384
  308.5 0.6 copy-start.13
  308.5 2.3 copy-start
  309.1 1.7 copy-start.11
  475.3 33.8 %copy-start.14 = (f32[2048]{0:T(1024)S(1)}, f32[2048]{0:T(1024)}, u32[]{:S(2)}) copy-start(f32[2048]{0:T(1024)} %copy-done.13) | copy-start | bytes 24580
  547.5 46.5 %copy-start.1 = (bf16[2048,1280]{1,0:T(8,128)(2,1)S(1)}, bf16[2048,1280]{1,0:T(8,128)(2,1)}, u32[]{:S(2)}) copy-start(bf16[2048,1280]{1,0:T(8,128)(2,1)} %copy-done) | copy-start | bytes 15728644
  547.5 46.5 %copy-start.12 = (f32[2048]{0:T(1024)S(1)}, f32[2048]{0:T(1024)}, u32[]{:S(2)}) copy-start(f32[2048]{0:T(1024)} %copy-done.11) | copy-start | bytes 24580
  848.3 76.2 %copy-start.2 = (bf16[2,40,4480]{2,1,0:T(8,128)(2,1)S(1)}, bf16[2,40,4480]{2,1,0:T(8,128)(2,1)}, u32[]{:S(2)}) copy-start(bf16[2,40,4480]{2,1,0:T(8,128)(2,1)} %param.13) | copy-start | bytes 2150404
  848.3 76.2 %copy-start.5 = (f32[2,40,4480]{2,1,0:T(8,128)S(1)}, f32[2,40,4480]{2,1,0:T(8,128)}, u32[]{:S(2)}) copy-start(f32[2,40,4480]{2,1,0:T(8,128)} %param.19) | copy-start | bytes 4300804
  848.3 76.2 %copy-start.6 = (f32[2,40,4480]{2,1,0:T(8,128)S(1)}, f32[2,40,4480]{2,1,0:T(8,128)}, u32[]{:S(2)}) copy-start(f32[2,40,4480]{2,1,0:T(8,128)} %param.16) | copy-start | bytes 4300804
  892.4 34.3 %copy-start.3 = (bf16[2,40,4480]{2,1,0:T(8,128)(2,1)S(1)}, bf16[2,40,4480]{2,1,0:T(8,128)(2,1)}, u32[]{:S(2)}) copy-start(bf16[2,40,4480]{2,1,0:T(8,128)(2,1)} %param.14) | copy-start | bytes 2150404
  916.1 10.6 %copy-start.7 = (f32[2,40,4480]{2,1,0:T(8,128)S(1)}, f32[2,40,4480]{2,1,0:T(8,128)}, u32[]{:S(2)}) copy-start(f32[2,40,4480]{2,1,0:T(8,128)} %param.20) | copy-start | bytes 4300804
  916.1 10.6 %copy-start.8 = (f32[2,40,4480]{2,1,0:T(8,128)S(1)}, f32[2,40,4480]{2,1,0:T(8,128)}, u32[]{:S(2)}) copy-start(f32[2,40,4480]{2,1,0:T(8,128)} %param.17) | copy-start | bytes 4300804
  918.3 10.6 %collective-permute-start.1 = (bf16[280,640]{1,0:T(8,128)(2,1)S(1)}, bf16[280,640]{1,0:T(8,128)(2,1)S(1)}, u32[]{:S(2)}, u32[]{:S(2)}) collective-permute-start(bf16[280,640]{1,0:T(8,128)(2,1)S(1)} %slice.65), channel_id=1, source_target_pairs={{0,1},{1,0},{2,3},{3,2},{4,5},{5,4},{6,7},{7,6},{8,9},{9,8},{10,11... | collective-permute-start | bytes 1075208 | tf_op jit(solution)/shard_map/ppermute | solution.py:416
  924.0 5.3 copy-start.4
  924.0 5.3 copy-start.9
  924.0 5.3 copy-start.10
  924.0 5.1 collective-permute-start
Sparse Core Ops, SparseCore 0:
  10.8 63.4 all-gather.12
  77.1 59.2 all-gather.16
  139.3 60.0 all-gather.18
  202.1 60.0 all-gather.14
  264.9 59.2 all-gather.20
  326.9 59.2 all-gather.22
